TPU v7x, 32 devices: a whole 2x2x4 slice. The times are simulated.
32 devices in a mesh: row: 2 (over x), col: 16 (over z, y, core).
Axes of the slice: x: 2, y: 2, z: 4, core: 2. Of those that a mesh axis runs over, the one named last changes fastest.
Arguments:
- upper_a: float32 [8, 2, 256, 16, 256], P(None, 'row', None, 'col'), may hold values from -0.375 to 0.375
- upper_b: float32 [8, 2, 256, 16, 256], P(None, 'row', None, 'col'), may hold values from -0.375 to 0.375
- right_side: float32 [8, 2, 256, 16, 256], P(None, 'row', None, 'col'), may hold values from -6 to 6
- vectors_a: float32 [8, 2, 256, 256], P(None, 'row'), may hold values from -0.375 to 0.375
- inverse_a: float32 [8, 2, 256, 256], P(None, 'row'), may hold values from -0.375 to 0.375
- values_a: float32 [8, 2, 256], P(None, 'row'), may hold values from 0.5 to 2
- vectors_b: float32 [16, 256, 256], P('col'), may hold values from -0.375 to 0.375
- inverse_b: float32 [16, 256, 256], P('col'), may hold values from -0.375 to 0.375
- values_b: float32 [16, 256], P('col'), may hold values from 0.5 to 2
Outputs:
- solved: float32 [8, 2, 256, 16, 256], P(None, 'row', None, 'col')
All inputs are finite; a program needn't handle non-finite values.
Results may differ from a plain program's by a relative error of at most 0.0001.
Values sent between devices are 32-bit elements; how exact they have to be, the bound alone decides.
A program may use at most 64 MiB of HBM per device.

v0:
```python
import jax
import jax.numpy as jnp
from jax import lax
from jax.sharding import PartitionSpec as P

FRONTS = 4
EXACT = lax.Precision.HIGHEST


def passed_along(value, axis, by):
    length = lax.axis_size(axis)
    pairs = [(i, i + by) for i in range(length) if 0 <= i + by < length]
    return lax.ppermute(value, axis, pairs)


def shifted(value, axis, steps):
    count = lax.axis_size(axis)
    pairs = [(source, (source + steps) % count) for source in range(count)]
    return lax.ppermute(value, axis, pairs)


def spread(value, axis, root):
    mine = lax.axis_index(axis) == root
    return lax.psum(jnp.where(mine, value, jnp.zeros_like(value)), axis)


def matmul(former, latter):
    return jnp.dot(former, latter, precision=EXACT, preferred_element_type=jnp.float32)


def diagonal_solve(residual, vectors_a, inverse_a, values_a, vectors_b, inverse_b, values_b):
    rotated = matmul(matmul(inverse_a, residual), vectors_b)
    scaled = rotated / (values_a[:, None] + values_b[None, :])
    return matmul(matmul(vectors_a, scaled), inverse_b)


def body(
    upper_a, upper_b, right_side, vectors_a, inverse_a, values_a, vectors_b, inverse_b, values_b
):
    row_count = lax.axis_size("row")
    col_count = lax.axis_size("col")
    row_pos = lax.axis_index("row")
    col_pos = lax.axis_index("col")
    local_blocks = right_side.shape[0]
    block_size = right_side.shape[2]
    square = (local_blocks, block_size, block_size)
    panel_a = upper_a.reshape(square)
    panel_b = upper_b.reshape(square)
    work = right_side.reshape(square)
    left_vectors = vectors_a.reshape(square)
    left_inverse = inverse_a.reshape(square)
    left_values = values_a.reshape(local_blocks, block_size)
    right_vectors = vectors_b.reshape(block_size, block_size)
    right_inverse = inverse_b.reshape(block_size, block_size)
    right_values = values_b.reshape(block_size)
    block_ids = jnp.arange(local_blocks, dtype=jnp.int32)
    global_rows = block_ids * row_count + row_pos
    offsets = list(range(-1, FRONTS - 1))
    moved_upper = {}
    for offset in offsets:
        if offset == 0:
            moved_upper[offset] = panel_a
        else:
            moved_upper[offset] = passed_along(panel_a, "col", offset)
    zero_block = jnp.zeros((1, block_size, block_size), jnp.float32)
    moved_lower = {}
    for offset in offsets:
        if offset % row_count == 0:
            arrived = panel_b
        else:
            arrived = shifted(panel_b, "row", -offset)
        block_carry = jnp.floor_divide(row_pos + offset, row_count)
        padded = jnp.concatenate([zero_block, arrived, zero_block], axis=0)
        moved_lower[offset] = lax.dynamic_slice_in_dim(padded, 1 + block_carry, local_blocks, 0)
    for offset in offsets:
        target = col_pos - offset
        slot_index = jnp.floor_divide(target - row_pos, row_count)
        present = (
            (jnp.remainder(target - row_pos, row_count) == 0) & (target >= 0) & (target < col_count)
        )
        picked = jnp.clip(slot_index, 0, local_blocks - 1)
        residual = lax.dynamic_index_in_dim(work, picked, 0, keepdims=False)
        solved = diagonal_solve(
            residual,
            lax.dynamic_index_in_dim(left_vectors, picked, 0, keepdims=False),
            lax.dynamic_index_in_dim(left_inverse, picked, 0, keepdims=False),
            lax.dynamic_index_in_dim(left_values, picked, 0, keepdims=False),
            right_vectors,
            right_inverse,
            right_values,
        )
        on_front = (block_ids == slot_index) & present
        work = jnp.where(on_front[:, None, None], solved[None], work)
        column_block = spread(solved, "row", jnp.remainder(target, row_count))
        upper_term = jnp.einsum("qab,bc->qac", moved_upper[offset], column_block, precision=EXACT)
        slot_blocks = jnp.where(on_front[:, None, None], solved[None], jnp.zeros_like(work))
        row_solved = lax.psum(slot_blocks, "col")
        lower_term = jnp.einsum("qab,qbc->qac", row_solved, moved_lower[offset], precision=EXACT)
        pending = col_pos - global_rows > offset
        work = jnp.where(pending[:, None, None], work - (upper_term + lower_term), work)
    return work.reshape(right_side.shape)


def solution(mesh):
    return jax.shard_map(
        body,
        mesh=mesh,
        in_specs=(
            P(None, "row", None, "col", None),
            P(None, "row", None, "col", None),
            P(None, "row", None, "col", None),
            P(None, "row", None, None),
            P(None, "row", None, None),
            P(None, "row", None),
            P("col", None, None),
            P("col", None, None),
            P("col", None),
        ),
        out_specs=P(None, "row", None, "col", None),
        check_vma=False,
    )
```

profile of v0, /device:TPU:0, one launch (start us, length us, event | category | flops | bytes accessed | tf_op | source)
XLA Modules:
  0.0 592.5 jit_solution(1330975827765755095)
XLA Ops:
  6.5 3.2 copy.54
  9.7 3.0 collective-permute-start.1
  12.7 1.5 copy.55
  14.3 1.4 collective-permute-start
  15.8 1.1 constant_dynamic-slice_fusion.4
  17.0 0.4 fusion.13
  17.4 0.4 convolution_divide_fusion.3
  17.8 1.3 fusion.41
  19.1 1.1 broadcast_select_fusion.7
  20.2 0.0 all-reduce.11.cloned.1.call-start
  20.3 0.1 copy.10
  20.5 1.7 broadcast_select_fusion.3
  22.2 0.0 all-reduce.11.cloned.1.call-update
  22.2 0.3 all-reduce.15.cloned.1.call-start
  22.5 6.0 %copy.11 = f32[8,1,256,1,256]{2,4,0,3,1:T(8,128)} copy(f32[8,1,256,1,256]{4,3,2,1,0:T(1,128)} %param.11) | data formatting | bytes 4194304 | tf_op args[2]
  28.6 35.7 %collective-permute-done.1 = f32[8,256,256]{2,1,0:T(8,128)} collective-permute-done((f32[8,256,256]{2,1,0:T(8,128)}, f32[8,256,256]{2,1,0:T(8,128)}, u32[]{:S(2)}, u32[]{:S(2)}) %collective-permute-start.1) | collective-permute-done | bytes 2097184 | tf_op jit(solution)/shard_map/ppermute | solution.py:19
  64.3 5.4 pad_maximum_fusion
  69.7 6.5 %fusion.26 = f32[256,8,256]{2,0,1:T(8,128)} fusion(f32[8,256,256]{2,1,0:T(8,128)} %collective-permute-done, f32[256,256]{1,0:T(8,128)} %all-reduce.9.cloned.1.call-done), kind=kOutput, calls=%fused_computation.45 | convolution fusion | flops 1610612736 | bytes 4456448 | tf_op jit(solution)/shard_map/qab,bc->qac/dot_general | solution.py:95
  76.2 77.0 %all-reduce.11.cloned.1.call-done = f32[8,256,256]{1,2,0:T(8,128)} async-done(((f32[8,256,256]{1,2,0:T(8,128)}), f32[8,256,256]{1,2,0:T(8,128)}) %all-reduce.11.cloned.1.call-update) | async-done | bytes 2097168 | tf_op jit(solution)/shard_map/psum | solution.py:97
  153.2 7.2 %subtract_select_fusion.3 = f32[8,256,256]{1,2,0:T(8,128)S(1)} fusion(f32[256,8,256]{2,0,1:T(8,128)} %fusion.26, f32[8,1,256,1,256]{2,4,0,3,1:T(8,128)} %copy.11, f32[8,256,256]{1,2,0:T(8,128)} %all-reduce.11.cloned.1.call-done, f32[10,256,256]{2,1,0:T(8,128)} %get-tuple-element.8, s32[]{:T(128)S(6)} %select_n.168, f32[256,256]{0,1:T(8,128)S(1)} %copy.10, ...), kind=kOutput, calls=%fused_computation.7 | convolution fusion | flops 1612709888 | bytes 10747924 | tf_op jit(solution)/shard_map/qab,qbc->qac/dot_general | solution.py:98
  160.4 1.3 copy-done.2
  161.7 0.4 fusion.24
  162.1 0.4 convolution_divide_fusion.2
  162.5 1.3 fusion.44
  163.9 1.1 broadcast_select_fusion.6
  164.9 0.1 copy.15
  165.1 1.7 broadcast_select_fusion.2
  166.8 0.0 all-reduce.15.cloned.1.call-update
  166.8 0.0 all-reduce.13.cloned.1.call-start
  166.9 2.7 collective-permute-start.2
  169.6 0.6 all-reduce.17.cloned.1.call-start
  170.2 98.3 %all-reduce.15.cloned.1.call-done = f32[8,256,256]{1,2,0:T(8,128)} async-done(((f32[8,256,256]{1,2,0:T(8,128)}), f32[8,256,256]{1,2,0:T(8,128)}) %all-reduce.15.cloned.1.call-update) | async-done | bytes 2097168 | tf_op jit(solution)/shard_map/psum | solution.py:97
  268.5 7.2 %fusion.5 = f32[8,256,256]{1,2,0:T(8,128)} fusion(f32[8,256,256]{1,2,0:T(8,128)} %all-reduce.15.cloned.1.call-done, f32[10,256,256]{2,1,0:T(8,128)} %get-tuple-element.7, s32[]{:T(128)S(6)} %select_n.176), kind=kOutput, calls=%fused_computation.20 | convolution fusion | flops 1610612736 | bytes 6291460 | tf_op jit(solution)/shard_map/qab,qbc->qac/dot_general | solution.py:98
  275.7 17.7 %all-reduce.13.cloned.1.call-done = f32[256,256]{1,0:T(8,128)} async-done(((f32[256,256]{1,0:T(8,128)}), f32[256,256]{1,0:T(8,128)}) %all-reduce.13.cloned.1.call-update) | async-done | bytes 262160 | tf_op jit(solution)/shard_map/psum | solution.py:24
  293.4 6.7 %subtract_select_fusion.2 = f32[8,256,256]{1,2,0:T(8,128)S(1)} fusion(f32[8,256,256]{1,2,0:T(8,128)} %fusion.5, f32[8,256,256]{1,2,0:T(8,128)} %copy-done.2, f32[256,256]{0,1:T(8,128)S(1)} %copy.15, pred[8]{0:T(512)(128)(4,1)S(1)} %compare_and_fusion.1, pred[8]{0:T(512)(128)(4,1)S(1)} %get-tuple-element.14, f32[256,256]{1,0:T(8,128)} %all-reduce.13.cloned.1.call-done, ...), kind=kOutput, calls=%fused_computation.6 | convolution fusion | flops 1612709888 | bytes 8912912 | tf_op jit(solution)/shard_map/qab,bc->qac/dot_general | solution.py:95
  300.2 1.3 copy-done.1
  301.4 0.4 fusion.21
  301.9 0.4 convolution_divide_fusion.1
  302.3 1.3 fusion.47
  303.6 1.1 broadcast_select_fusion.5
  304.7 0.1 copy.19
  304.8 0.0 all-reduce.17.cloned.1.call-update
  304.8 0.0 all-reduce.19.cloned.1.call-start
  304.9 1.6 broadcast_select_fusion.1
  306.5 0.0 all-reduce.23.cloned.1.call-start
  306.5 4.9 collective-permute-start.3
  311.5 16.8 %all-reduce.17.cloned.1.call-done = f32[256,256]{1,0:T(8,128)} async-done(((f32[256,256]{1,0:T(8,128)}), f32[256,256]{1,0:T(8,128)}) %all-reduce.17.cloned.1.call-update) | async-done | bytes 262160 | tf_op jit(solution)/shard_map/psum | solution.py:24
  328.3 6.5 %fusion.19 = f32[256,8,256]{2,0,1:T(8,128)} fusion(f32[8,256,256]{2,1,0:T(8,128)} %collective-permute-done.2, f32[256,256]{1,0:T(8,128)} %all-reduce.17.cloned.1.call-done), kind=kOutput, calls=%fused_computation.38 | convolution fusion | flops 1610612736 | bytes 4456448 | tf_op jit(solution)/shard_map/qab,bc->qac/dot_general | solution.py:95
  334.8 100.3 %all-reduce.19.cloned.1.call-done = f32[8,256,256]{1,2,0:T(8,128)} async-done(((f32[8,256,256]{1,2,0:T(8,128)}), f32[8,256,256]{1,2,0:T(8,128)}) %all-reduce.19.cloned.1.call-update) | async-done | bytes 2097168 | tf_op jit(solution)/shard_map/psum | solution.py:97
  435.1 7.2 %subtract_select_fusion.1 = f32[8,256,256]{1,2,0:T(8,128)S(1)} fusion(f32[256,8,256]{2,0,1:T(8,128)} %fusion.19, f32[8,256,256]{1,2,0:T(8,128)} %copy-done.1, f32[8,256,256]{1,2,0:T(8,128)} %all-reduce.19.cloned.1.call-done, f32[10,256,256]{2,1,0:T(8,128)} %get-tuple-element.8, s32[]{:T(128)S(6)} %select_n.184, f32[256,256]{0,1:T(8,128)S(1)} %copy.19, ...), kind=kOutput, calls=%fused_computation.5 | convolution fusion | flops 1612709888 | bytes 10747924 | tf_op jit(solution)/shard_map/qab,qbc->qac/dot_general | solution.py:98
  442.3 1.3 copy-done.3
  443.7 0.4 fusion.17
  444.1 0.4 convolution_divide_fusion
  444.5 1.3 fusion.50
  445.8 1.1 broadcast_select_fusion.4
  446.9 0.1 copy.23
  447.0 1.5 broadcast_select_fusion
  448.6 0.3 all-reduce.21.cloned.1.call-start
  448.9 0.5 all-reduce.21.cloned.1.call-update
  449.3 97.0 %all-reduce.23.cloned.1.call-done = f32[8,256,256]{1,2,0:T(8,128)} async-done(((f32[8,256,256]{1,2,0:T(8,128)}), f32[8,256,256]{1,2,0:T(8,128)}) %all-reduce.23.cloned.1.call-update) | async-done | bytes 2097168 | tf_op jit(solution)/shard_map/psum | solution.py:97
  546.4 7.0 %fusion.1 = f32[8,256,256]{1,2,0:T(8,128)} fusion(f32[8,256,256]{1,2,0:T(8,128)} %all-reduce.23.cloned.1.call-done, f32[10,256,256]{2,1,0:T(8,128)} %get-tuple-element.7, s32[]{:T(128)S(6)} %select_n.192), kind=kOutput, calls=%fused_computation.16 | convolution fusion | flops 1610612736 | bytes 6291460 | tf_op jit(solution)/shard_map/qab,qbc->qac/dot_general | solution.py:98
  553.4 18.0 %all-reduce.21.cloned.1.call-done = f32[256,256]{1,0:T(8,128)} async-done(((f32[256,256]{1,0:T(8,128)}), f32[256,256]{1,0:T(8,128)}) %all-reduce.21.cloned.1.call-update) | async-done | bytes 262160 | tf_op jit(solution)/shard_map/psum | solution.py:24
  571.5 8.0 %fusion = f32[8,1,256,1,256]{2,4,0,3,1:T(8,128)} fusion(f32[8,256,256]{1,2,0:T(8,128)} %fusion.1, f32[8,256,256]{1,2,0:T(8,128)} %copy-done.3, f32[8,256,256]{2,1,0:T(8,128)} %collective-permute-done.3, f32[256,256]{0,1:T(8,128)S(1)} %copy.23, pred[8]{0:T(512)(128)(4,1)S(1)} %compare_and_fusion.3, pred[8]{0:T(512)(128)(4,1)S(1)} %get-tuple-element.5, ...), kind=kOutput, calls=%fused_computation.8 | convolution fusion | flops 1612709888 | bytes 8912912 | tf_op jit(solution)/shard_map/qab,bc->qac/dot_general | solution.py:95
  579.4 6.0 %copy.27 = f32[8,1,256,1,256]{4,3,2,1,0:T(1,128)} copy(f32[8,1,256,1,256]{2,4,0,3,1:T(8,128)} %fusion) | data formatting | bytes 4194304 | tf_op jit(solution)/shard_map/reshape | solution.py:101
  (32 shorter events, 0.2 us)
Async XLA Ops:
  6.5 10.4 %copy-start = (f32[8,1,256,256]{3,2,1,0:T(8,128)S(1)}, f32[8,1,256,256]{3,2,1,0:T(8,128)}, u32[]{:S(2)}) copy-start(f32[8,1,256,256]{3,2,1,0:T(8,128)} %param.13) | copy-start | bytes 6291460
  6.5 63.1 %all-reduce.9.cloned.1.call-start = ((), (), s32[]{:S(2)}) async-start(), calls=%async_computation | async-start | bytes 524288 | tf_op jit(solution)/shard_map/psum | solution.py:24
  6.5 6.2 %copy-start.4 = (f32[8,1,256,1,256]{4,3,2,1,0:T(1,128)S(1)}, f32[8,1,256,1,256]{4,3,2,1,0:T(1,128)}, u32[]{:S(2)}) copy-start(f32[8,1,256,1,256]{4,3,2,1,0:T(1,128)} %param.9) | copy-start | bytes 6291460
  9.7 7.2 %copy-start.6 = (f32[8,1,256]{2,1,0:T(1,128)S(1)}, f32[8,1,256]{2,1,0:T(1,128)}, u32[]{:S(2)}) copy-start(f32[8,1,256]{2,1,0:T(1,128)} %param.14) | copy-start | bytes 24580
  9.7 7.6 %copy-start.7 = (f32[1,256,256]{2,1,0:T(8,128)S(1)}, f32[1,256,256]{2,1,0:T(8,128)}, u32[]{:S(2)}) copy-start(f32[1,256,256]{2,1,0:T(8,128)} %param.15) | copy-start | bytes 786436
  9.7 7.7 %copy-start.8 = (f32[1,256]{1,0:T(1,128)S(1)}, f32[1,256]{1,0:T(1,128)}, u32[]{:S(2)}) copy-start(f32[1,256]{1,0:T(1,128)} %param.17) | copy-start | bytes 3076
  9.7 54.5 %collective-permute-start.1 = (f32[8,256,256]{2,1,0:T(8,128)}, f32[8,256,256]{2,1,0:T(8,128)}, u32[]{:S(2)}, u32[]{:S(2)}) collective-permute-start(f32[8,256,256]{2,1,0:T(8,128)} %bitcast.125), channel_id=1, source_target_pairs={{0,16},{16,0},{1,17},{17,1},{2,18},{18,2},{3,19},{19,3},{4,20},{20... | collective-permute-start | bytes 6291464 | tf_op jit(solution)/shard_map/ppermute | solution.py:19
  14.3 4.9 copy-start.5
  14.3 55.4 %collective-permute-start = (f32[8,256,256]{2,1,0:T(8,128)}, f32[8,256,256]{2,1,0:T(8,128)}, u32[]{:S(2)}, u32[]{:S(2)}) collective-permute-start(f32[8,256,256]{2,1,0:T(8,128)} %bitcast.126), channel_id=1, source_target_pairs={{1,0},{2,1},{3,2},{4,3},{5,4},{6,5},{7,6},{8,7},{9,8},{10,9},{11,1... | collective-permute-start | bytes 6291464 | tf_op jit(solution)/shard_map/ppermute | solution.py:13
  20.2 132.9 %all-reduce.11.cloned.1.call-start = ((), (), s32[]{:S(2)}) async-start(), calls=%async_computation.1 | async-start | bytes 4194304 | tf_op jit(solution)/shard_map/psum | solution.py:97
  22.2 246.3 %all-reduce.15.cloned.1.call-start = ((), (), s32[]{:S(2)}) async-start(), calls=%async_computation.3 | async-start | bytes 4194304 | tf_op jit(solution)/shard_map/psum | solution.py:97
  160.4 1.4 copy-start.2
  166.8 126.6 %all-reduce.13.cloned.1.call-start = ((), (), s32[]{:S(2)}) async-start(), calls=%async_computation.2 | async-start | bytes 524288 | tf_op jit(solution)/shard_map/psum | solution.py:24
  166.9 144.6 %collective-permute-start.2 = (f32[8,256,256]{2,1,0:T(8,128)}, f32[8,256,256]{2,1,0:T(8,128)}, u32[]{:S(2)}, u32[]{:S(2)}) collective-permute-start(f32[8,256,256]{2,1,0:T(8,128)} %bitcast.126), channel_id=1, source_target_pairs={{0,1},{1,2},{2,3},{3,4},{4,5},{5,6},{6,7},{7,8},{8,9},{9,10},{10,1... | collective-permute-start | bytes 6291464 | tf_op jit(solution)/shard_map/ppermute | solution.py:13
  169.6 158.7 %all-reduce.17.cloned.1.call-start = ((), (), s32[]{:S(2)}) async-start(), calls=%async_computation.4 | async-start | bytes 524288 | tf_op jit(solution)/shard_map/psum | solution.py:24
  300.1 1.3 copy-start.1
  304.8 130.2 %all-reduce.19.cloned.1.call-start = ((), (), s32[]{:S(2)}) async-start(), calls=%async_computation.5 | async-start | bytes 4194304 | tf_op jit(solution)/shard_map/psum | solution.py:97
  306.5 239.9 %all-reduce.23.cloned.1.call-start = ((), (), s32[]{:S(2)}) async-start(), calls=%async_computation.7 | async-start | bytes 4194304 | tf_op jit(solution)/shard_map/psum | solution.py:97
  306.5 246.9 %collective-permute-start.3 = (f32[8,256,256]{2,1,0:T(8,128)}, f32[8,256,256]{2,1,0:T(8,128)}, u32[]{:S(2)}, u32[]{:S(2)}) collective-permute-start(f32[8,256,256]{2,1,0:T(8,128)} %bitcast.126), channel_id=1, source_target_pairs={{0,2},{1,3},{2,4},{3,5},{4,6},{5,7},{6,8},{7,9},{8,10},{9,11},{10,... | collective-permute-start | bytes 6291464 | tf_op jit(solution)/shard_map/ppermute | solution.py:13
  442.3 1.4 copy-start.3
  448.6 122.9 %all-reduce.21.cloned.1.call-start = ((), (), s32[]{:S(2)}) async-start(), calls=%async_computation.6 | async-start | bytes 524288 | tf_op jit(solution)/shard_map/psum | solution.py:24
Sparse Core Ops, SparseCore 0:
  20.4 31.0 all-reduce.8
  55.0 98.1 all-reduce.10
  166.9 101.5 all-reduce.14
  270.6 22.7 all-reduce.12
  305.0 23.2 all-reduce.16
  331.7 103.3 all-reduce.18
  448.7 97.6 all-reduce.22
  548.7 22.7 all-reduce.20
where the time goes:
time: 596 us; the launch traced here: 592 us
  waiting for transfers between devices  462 us (78%)
  matrix products  69 us (12%)
  local copies, waits for them, and re-layouts  22.5 us (4%)
  between operations  14.2 us (2%)
  starting transfers between devices  13.3 us (2%)
  other arithmetic  11.9 us (2%)
    psum x4, waiting for transfers between devices, body(): row_solved = lax.psum(slot_blocks, 'col')  373 us
    psum x4, waiting for transfers between devices, spread(): return lax.psum(jnp.where(mine, value, jnp.zeros_like(value)), axis)  52.6 us
    ppermute x1, waiting for transfers between devices, shifted(): return lax.ppermute(value, axis, pairs)  35.7 us
    dot_general x4, matrix products, body(): jnp.einsum('qab,qbc->qac', row_solved, moved_lower[offset], precision=EXACT)  28.6 us
    dot_general x4, matrix products, body(): jnp.einsum('qab,bc->qac', moved_upper[offset], column_block, precision=EX...  27.6 us
    unnamed x21, local copies, waits for them, and re-layouts  14.8 us
    dot_general x16, matrix products, matmul(): jnp.dot(former, latter, precision=EXACT, preferred_element_type=jnp.float32)  12.8 us
  transfers between devices with their start and end apart: 12, of which 8 were waited for; matrix products, arithmetic and copies ran while one was open for 12% of the time, Pallas kernels for 0%

commit v1 on v0

--- a/solution.py
+++ b/solution.py
@@ -21,7 +21,7 @@
 
 def spread(value, axis, root):
     mine = lax.axis_index(axis) == root
-    return lax.psum(jnp.where(mine, value, jnp.zeros_like(value)), axis)
+    return jnp.sum(lax.all_gather(jnp.where(mine, value, jnp.zeros_like(value)), axis), axis=0)
 
 
 def matmul(former, latter):

time: 596 us -> 499 us (0.84)
  waiting for transfers between devices: 462 us -> 305 us
  blocking collectives: 0 us -> 71.8 us
  matrix products: 69 us -> 59.7 us
    all_gather x0 -> x4, blocking collectives: none -> 71.8 us  [spread(): lax.all_gather(jnp.where(mine, value, jnp.zeros_like(value)), axis)]
    psum x4, waiting for transfers between devices: 373 us -> 304 us  [body(): row_solved = lax.psum(slot_blocks, 'col')]
    psum x4 -> x0, waiting for transfers between devices: 52.6 us -> none  [spread(): return lax.psum(jnp.where(mine, value, jnp.zeros_like(value)), axis)]
    ppermute x1, waiting for transfers between devices: 35.7 us -> 0.01 us  [shifted(): return lax.ppermute(value, axis, pairs)]
    unnamed x21 -> x33, local copies, waits for them, and re-layouts: 14.8 us -> 14.8 us
  transfers between devices with their start and end apart: 12 -> 8, of which waited for: 8 -> 4; matrix products, arithmetic and copies ran while one was open for 12% -> 13% of each run, Pallas kernels for 0% -> 0%
where the time goes in v1:
time: 499 us; the launch traced here: 496 us
  waiting for transfers between devices  305 us (61%)
  blocking collectives  71.8 us (14%)
  matrix products  59.7 us (12%)
  local copies, waits for them, and re-layouts  22.5 us (5%)
  between operations  13.9 us (3%)
  other arithmetic  12 us (2%)
  starting transfers between devices  11.6 us (2%)
    psum x4, waiting for transfers between devices, body(): row_solved = lax.psum(slot_blocks, 'col')  304 us
    all_gather x4, blocking collectives, spread(): lax.all_gather(jnp.where(mine, value, jnp.zeros_like(value)), axis)  71.8 us
    dot_general x4, matrix products, body(): jnp.einsum('qab,qbc->qac', row_solved, moved_lower[offset], precision=EXACT)  26.2 us
    dot_general x4, matrix products, body(): jnp.einsum('qab,bc->qac', moved_upper[offset], column_block, precision=EX...  23.5 us
    unnamed x33, local copies, waits for them, and re-layouts  14.8 us
    dot_general x16, matrix products, matmul(): jnp.dot(former, latter, precision=EXACT, preferred_element_type=jnp.float32)  9.98 us
  transfers between devices with their start and end apart: 8, of which 4 were waited for; matrix products, arithmetic and copies ran while one was open for 13% of the time, Pallas kernels for 0%

profile of v1, /device:TPU:0, one launch (start us, length us, event | category | flops | bytes accessed | tf_op | source)
XLA Modules:
  0.0 496.1 jit_solution(17231671994000134515)
XLA Ops:
  6.5 3.2 copy.69
  9.7 1.4 collective-permute-start
  11.2 1.5 copy.68
  12.7 3.0 collective-permute-start.1
  15.7 1.1 constant_dynamic-slice_fusion.4
  16.8 0.4 fusion.13
  17.4 0.4 convolution_divide_fusion.3
  17.8 1.3 fusion.41
  19.1 0.4 broadcast_select_fusion.7
  19.5 0.1 copy.24
  19.7 1.7 broadcast_select_fusion.3
  21.4 0.0 all-reduce.5.cloned.1.call-update
  21.4 0.0 all-reduce.7.cloned.1.call-start
  21.4 46.1 %all-gather = f32[512,256]{1,0:T(8,128)S(1)} all-gather(f32[256,256]{1,0:T(8,128)S(1)} %get-tuple-element.16), channel_id=2, replica_groups=mesh['row'=2,'col'=16] {'row'}, dimensions={0}, use_global_device_ids=true | all-gather | bytes 786432 | tf_op jit(solution)/shard_map/all_gather | solution.py:24
  67.6 6.0 %copy.25 = f32[8,1,256,1,256]{2,4,0,3,1:T(8,128)} copy(f32[8,1,256,1,256]{4,3,2,1,0:T(1,128)} %param.11) | data formatting | bytes 4194304 | tf_op args[2]
  73.7 0.0 collective-permute-done.1
  73.7 5.3 %pad_maximum_fusion = (f32[10,256,256]{2,1,0:T(8,128)}, f32[10,256,256]{2,1,0:T(8,128)}) fusion(f32[1,256,256]{2,1,0:T(8,128)S(1)} %broadcast_in_dim.129, f32[8,256,256]{2,1,0:T(8,128)} %bitcast.129, f32[8,256,256]{2,1,0:T(8,128)} %collective-permute-done.1), kind=kLoop, calls=%fused_computation | loop fusion | flops 2621440 | bytes 9699328 | tf_op jit(solution)/shard_map/concatenate | solution.py:73
  79.0 0.0 collective-permute-done
  79.0 6.4 %fusion.26 = f32[256,8,256]{2,0,1:T(8,128)} fusion(f32[8,256,256]{2,1,0:T(8,128)} %collective-permute-done, f32[256,256]{1,0:T(8,128)S(1)} %reduce_sum.36), kind=kOutput, calls=%fused_computation.45 | convolution fusion | flops 1610612736 | bytes 4456448 | tf_op jit(solution)/shard_map/qab,bc->qac/dot_general | solution.py:95
  85.4 37.8 %all-reduce.5.cloned.1.call-done = f32[8,256,256]{1,2,0:T(8,128)} async-done(((f32[8,256,256]{1,2,0:T(8,128)}), f32[8,256,256]{1,2,0:T(8,128)}) %all-reduce.5.cloned.1.call-update) | async-done | bytes 2097168 | tf_op jit(solution)/shard_map/psum | solution.py:97
  123.2 7.2 %subtract_select_fusion.3 = f32[8,256,256]{1,2,0:T(8,128)S(1)} fusion(f32[256,8,256]{2,0,1:T(8,128)} %fusion.26, f32[8,1,256,1,256]{2,4,0,3,1:T(8,128)} %copy.25, f32[8,256,256]{1,2,0:T(8,128)} %all-reduce.5.cloned.1.call-done, f32[10,256,256]{2,1,0:T(8,128)} %get-tuple-element.8, s32[]{:T(128)S(6)} %select_n.168, f32[256,256]{0,1:T(8,128)S(1)} %copy.24, ...), kind=kOutput, calls=%fused_computation.7 | convolution fusion | flops 1612709888 | bytes 10747924 | tf_op jit(solution)/shard_map/qab,qbc->qac/dot_general | solution.py:98
  130.4 1.3 copy-done.2
  131.8 0.4 fusion.24
  132.2 0.4 convolution_divide_fusion.2
  132.6 1.3 fusion.44
  133.9 0.4 broadcast_select_fusion.6
  134.3 0.1 copy.29
  134.5 1.7 broadcast_select_fusion.2
  136.2 0.0 all-reduce.7.cloned.1.call-update
  136.2 0.0 all-reduce.9.cloned.1.call-start
  136.2 2.7 collective-permute-start.2
  139.0 9.9 %all-gather.1 = f32[512,256]{1,0:T(8,128)S(1)} all-gather(f32[256,256]{1,0:T(8,128)S(1)} %get-tuple-element.18), channel_id=3, replica_groups=mesh['row'=2,'col'=16] {'row'}, dimensions={0}, use_global_device_ids=true | all-gather | bytes 786432 | tf_op jit(solution)/shard_map/all_gather | solution.py:24
  148.9 89.0 %all-reduce.7.cloned.1.call-done = f32[8,256,256]{1,2,0:T(8,128)} async-done(((f32[8,256,256]{1,2,0:T(8,128)}), f32[8,256,256]{1,2,0:T(8,128)}) %all-reduce.7.cloned.1.call-update) | async-done | bytes 2097168 | tf_op jit(solution)/shard_map/psum | solution.py:97
  237.9 5.9 %fusion.5 = f32[8,256,256]{1,2,0:T(8,128)S(1)} fusion(f32[8,256,256]{1,2,0:T(8,128)} %all-reduce.7.cloned.1.call-done, f32[10,256,256]{2,1,0:T(8,128)} %get-tuple-element.7, s32[]{:T(128)S(6)} %select_n.176), kind=kOutput, calls=%fused_computation.20 | convolution fusion | flops 1610612736 | bytes 6291460 | tf_op jit(solution)/shard_map/qab,qbc->qac/dot_general | solution.py:98
  243.8 0.0 copy-start.12
  243.8 3.9 subtract_select_fusion.2
  247.8 1.3 copy-done.1
  249.1 0.4 fusion.21
  249.5 0.4 convolution_divide_fusion.1
  249.9 1.3 fusion.47
  251.2 0.4 broadcast_select_fusion.5
  251.6 0.1 copy.33
  251.7 1.6 broadcast_select_fusion.1
  253.3 0.0 all-reduce.9.cloned.1.call-update
  253.3 0.0 all-reduce.11.cloned.1.call-start
  253.4 4.4 collective-permute-start.3
  257.8 7.4 %all-gather.2 = f32[512,256]{1,0:T(8,128)S(1)} all-gather(f32[256,256]{1,0:T(8,128)S(1)} %get-tuple-element.20), channel_id=4, replica_groups=mesh['row'=2,'col'=16] {'row'}, dimensions={0}, use_global_device_ids=true | all-gather | bytes 786432 | tf_op jit(solution)/shard_map/all_gather | solution.py:24
  265.3 0.0 collective-permute-done.2
  265.3 6.4 %fusion.19 = f32[256,8,256]{2,0,1:T(8,128)} fusion(f32[8,256,256]{2,1,0:T(8,128)} %collective-permute-done.2, f32[256,256]{1,0:T(8,128)S(1)} %reduce_sum.38), kind=kOutput, calls=%fused_computation.38 | convolution fusion | flops 1610612736 | bytes 4456448 | tf_op jit(solution)/shard_map/qab,bc->qac/dot_general | solution.py:95
  271.6 88.3 %all-reduce.9.cloned.1.call-done = f32[8,256,256]{1,2,0:T(8,128)} async-done(((f32[8,256,256]{1,2,0:T(8,128)}), f32[8,256,256]{1,2,0:T(8,128)}) %all-reduce.9.cloned.1.call-update) | async-done | bytes 2097168 | tf_op jit(solution)/shard_map/psum | solution.py:97
  360.0 7.2 %subtract_select_fusion.1 = f32[8,256,256]{1,2,0:T(8,128)S(1)} fusion(f32[256,8,256]{2,0,1:T(8,128)} %fusion.19, f32[8,256,256]{1,2,0:T(8,128)} %copy-done.1, f32[8,256,256]{1,2,0:T(8,128)} %all-reduce.9.cloned.1.call-done, f32[10,256,256]{2,1,0:T(8,128)} %get-tuple-element.8, s32[]{:T(128)S(6)} %select_n.184, f32[256,256]{0,1:T(8,128)S(1)} %copy.33, ...), kind=kOutput, calls=%fused_computation.5 | convolution fusion | flops 1612709888 | bytes 10747924 | tf_op jit(solution)/shard_map/qab,qbc->qac/dot_general | solution.py:98
  367.2 1.3 copy-done.4
  368.6 0.4 fusion.17
  369.0 0.4 convolution_divide_fusion
  369.4 1.3 fusion.50
  370.7 0.4 broadcast_select_fusion.4
  371.1 0.1 copy.37
  371.2 1.6 broadcast_select_fusion
  372.8 0.0 all-reduce.11.cloned.1.call-update
  372.8 8.3 %all-gather.3 = f32[512,256]{1,0:T(8,128)S(1)} all-gather(f32[256,256]{1,0:T(8,128)S(1)} %get-tuple-element.22), channel_id=5, replica_groups=mesh['row'=2,'col'=16] {'row'}, dimensions={0}, use_global_device_ids=true | all-gather | bytes 786432 | tf_op jit(solution)/shard_map/all_gather | solution.py:24
  381.2 89.4 %all-reduce.11.cloned.1.call-done = f32[8,256,256]{1,2,0:T(8,128)} async-done(((f32[8,256,256]{1,2,0:T(8,128)}), f32[8,256,256]{1,2,0:T(8,128)}) %all-reduce.11.cloned.1.call-update) | async-done | bytes 2097168 | tf_op jit(solution)/shard_map/psum | solution.py:97
  470.6 5.9 %fusion.1 = f32[8,256,256]{1,2,0:T(8,128)S(1)} fusion(f32[8,256,256]{1,2,0:T(8,128)} %all-reduce.11.cloned.1.call-done, f32[10,256,256]{2,1,0:T(8,128)} %get-tuple-element.7, s32[]{:T(128)S(6)} %select_n.192), kind=kOutput, calls=%fused_computation.16 | convolution fusion | flops 1610612736 | bytes 6291460 | tf_op jit(solution)/shard_map/qab,qbc->qac/dot_general | solution.py:98
  476.5 6.8 %fusion = f32[8,1,256,1,256]{2,4,0,3,1:T(8,128)} fusion(f32[8,256,256]{1,2,0:T(8,128)S(1)} %fusion.1, f32[8,256,256]{1,2,0:T(8,128)S(1)} %copy-done.5, f32[8,256,256]{2,1,0:T(8,128)} %collective-permute-done.3, f32[256,256]{0,1:T(8,128)S(1)} %copy.37, pred[8]{0:T(512)(128)(4,1)S(1)} %compare_and_fusion.3, pred[8]{0:T(512)(128)(4,1)S(1)} %get-tuple-element.5, ...), kind=kOutput, calls=%fused_computation.8 | convolution fusion | flops 1612709888 | bytes 8912912 | tf_op jit(solution)/shard_map/qab,bc->qac/dot_general | solution.py:95
  483.3 6.0 %copy.41 = f32[8,1,256,1,256]{4,3,2,1,0:T(1,128)} copy(f32[8,1,256,1,256]{2,4,0,3,1:T(8,128)} %fusion) | data formatting | bytes 4194304 | tf_op jit(solution)/shard_map/reshape | solution.py:101
  (40 shorter events, 0.3 us)
Async XLA Ops:
  6.5 10.3 %copy-start = (f32[8,1,256,256]{3,2,1,0:T(8,128)S(1)}, f32[8,1,256,256]{3,2,1,0:T(8,128)}, u32[]{:S(2)}) copy-start(f32[8,1,256,256]{3,2,1,0:T(8,128)} %param.13) | copy-start | bytes 6291460
  6.5 116.6 %all-reduce.5.cloned.1.call-start = ((), (), s32[]{:S(2)}) async-start(), calls=%async_computation | async-start | bytes 4194304 | tf_op jit(solution)/shard_map/psum | solution.py:97
  6.5 4.6 copy-start.8
  9.7 7.6 %copy-start.9 = (f32[8,1,256]{2,1,0:T(1,128)S(1)}, f32[8,1,256]{2,1,0:T(1,128)}, u32[]{:S(2)}) copy-start(f32[8,1,256]{2,1,0:T(1,128)} %param.14) | copy-start | bytes 24580
  9.7 7.6 %copy-start.10 = (f32[1,256,256]{2,1,0:T(8,128)S(1)}, f32[1,256,256]{2,1,0:T(8,128)}, u32[]{:S(2)}) copy-start(f32[1,256,256]{2,1,0:T(8,128)} %param.15) | copy-start | bytes 786436
  9.7 7.6 %copy-start.14 = (f32[1,256]{1,0:T(1,128)S(1)}, f32[1,256]{1,0:T(1,128)}, u32[]{:S(2)}) copy-start(f32[1,256]{1,0:T(1,128)} %param.17) | copy-start | bytes 3076
  9.7 69.3 %collective-permute-start = (f32[8,256,256]{2,1,0:T(8,128)}, f32[8,256,256]{2,1,0:T(8,128)}, u32[]{:S(2)}, u32[]{:S(2)}) collective-permute-start(f32[8,256,256]{2,1,0:T(8,128)} %bitcast.130), channel_id=1, source_target_pairs={{1,0},{2,1},{3,2},{4,3},{5,4},{6,5},{7,6},{8,7},{9,8},{10,9},{11,1... | collective-permute-start | bytes 6291464 | tf_op jit(solution)/shard_map/ppermute | solution.py:13
  12.7 6.4 %copy-start.7 = (f32[1,256,256]{2,1,0:T(8,128)S(1)}, f32[1,256,256]{2,1,0:T(8,128)}, u32[]{:S(2)}) copy-start(f32[1,256,256]{2,1,0:T(8,128)} %param.16) | copy-start | bytes 786436
  12.7 61.0 %collective-permute-start.1 = (f32[8,256,256]{2,1,0:T(8,128)}, f32[8,256,256]{2,1,0:T(8,128)}, u32[]{:S(2)}, u32[]{:S(2)}) collective-permute-start(f32[8,256,256]{2,1,0:T(8,128)} %bitcast.129), channel_id=1, source_target_pairs={{0,16},{16,0},{1,17},{17,1},{2,18},{18,2},{3,19},{19,3},{4,20},{20... | collective-permute-start | bytes 6291464 | tf_op jit(solution)/shard_map/ppermute | solution.py:19
  21.4 216.5 %all-reduce.7.cloned.1.call-start = ((), (), s32[]{:S(2)}) async-start(), calls=%async_computation.1 | async-start | bytes 4194304 | tf_op jit(solution)/shard_map/psum | solution.py:97
  123.2 9.0 %copy-start.11 = (f32[1,256,256]{2,1,0:T(8,128)S(1)}, f32[1,256,256]{2,1,0:T(8,128)}, u32[]{:S(2)}) copy-start(f32[1,256,256]{2,1,0:T(8,128)} %param.15) | copy-start | bytes 786436
  130.4 1.4 copy-start.2
  136.2 223.8 %all-reduce.9.cloned.1.call-start = ((), (), s32[]{:S(2)}) async-start(), calls=%async_computation.2 | async-start | bytes 4194304 | tf_op jit(solution)/shard_map/psum | solution.py:97
  136.2 129.0 %collective-permute-start.2 = (f32[8,256,256]{2,1,0:T(8,128)}, f32[8,256,256]{2,1,0:T(8,128)}, u32[]{:S(2)}, u32[]{:S(2)}) collective-permute-start(f32[8,256,256]{2,1,0:T(8,128)} %bitcast.130), channel_id=1, source_target_pairs={{0,1},{1,2},{2,3},{3,4},{4,5},{5,6},{6,7},{7,8},{8,9},{9,10},{10,1... | collective-permute-start | bytes 6291464 | tf_op jit(solution)/shard_map/ppermute | solution.py:13
  237.9 5.9 %copy-start.3 = (f32[8,256,256]{1,2,0:T(8,128)S(1)}, f32[8,256,256]{1,2,0:T(8,128)}, u32[]{:S(2)}) copy-start(f32[8,256,256]{1,2,0:T(8,128)} %copy-done.2) | copy-start | bytes 6291460
  237.9 5.9 %copy-start.6 = (f32[8,1,256,1,256]{4,3,2,1,0:T(1,128)S(1)}, f32[8,1,256,1,256]{4,3,2,1,0:T(1,128)}, u32[]{:S(2)}) copy-start(f32[8,1,256,1,256]{4,3,2,1,0:T(1,128)} %param.9) | copy-start | bytes 6291460
  243.8 5.7 %copy-start.12 = (f32[1,256,256]{2,1,0:T(8,128)S(1)}, f32[1,256,256]{2,1,0:T(8,128)}, u32[]{:S(2)}) copy-start(f32[1,256,256]{2,1,0:T(8,128)} %param.15) | copy-start | bytes 786436
  247.7 1.3 copy-start.1
  253.3 217.3 %all-reduce.11.cloned.1.call-start = ((), (), s32[]{:S(2)}) async-start(), calls=%async_computation.3 | async-start | bytes 4194304 | tf_op jit(solution)/shard_map/psum | solution.py:97
  253.4 223.1 %collective-permute-start.3 = (f32[8,256,256]{2,1,0:T(8,128)}, f32[8,256,256]{2,1,0:T(8,128)}, u32[]{:S(2)}, u32[]{:S(2)}) collective-permute-start(f32[8,256,256]{2,1,0:T(8,128)} %bitcast.130), channel_id=1, source_target_pairs={{0,2},{1,3},{2,4},{3,5},{4,6},{5,7},{6,8},{7,9},{8,10},{9,11},{10,... | collective-permute-start | bytes 6291464 | tf_op jit(solution)/shard_map/ppermute | solution.py:13
  360.0 9.0 %copy-start.13 = (f32[1,256,256]{2,1,0:T(8,128)S(1)}, f32[1,256,256]{2,1,0:T(8,128)}, u32[]{:S(2)}) copy-start(f32[1,256,256]{2,1,0:T(8,128)} %param.15) | copy-start | bytes 786436
  367.2 1.3 copy-start.4
  470.6 5.9 %copy-start.5 = (f32[8,256,256]{1,2,0:T(8,128)S(1)}, f32[8,256,256]{1,2,0:T(8,128)}, u32[]{:S(2)}) copy-start(f32[8,256,256]{1,2,0:T(8,128)} %copy-done.4) | copy-start | bytes 6291460
Sparse Core Ops, SparseCore 0:
  21.5 101.6 all-reduce.4
  136.3 101.5 all-reduce.6
  253.4 106.4 all-reduce.8
  373.0 97.5 all-reduce.10
